TPU v7x, 32 devices: a whole 2x2x4 slice. The times are simulated.
32 devices in a mesh: replica: 4 (over x, core), fsdp: 8 (over z, y).
Axes of the slice: x: 2, y: 2, z: 4, core: 2. Of those that a mesh axis runs over, the one named last changes fastest.
Arguments:
- anchor: float32 [1536, 1536], P('fsdp', 'replica'), may hold values from -0.15625 to 0.15625
- momentum: float32 [1536, 1536], P('fsdp', 'replica'), may hold values from -0.75 to 0.75
- change: float32 [4, 1536, 1536], P('replica', 'fsdp'), may hold values from -0.75 to 0.75
- adam_first: float32 [4, 1536, 1536], P('replica', 'fsdp'), may hold values from -4 to 4
- adam_second: float32 [4, 1536, 1536], P('replica', 'fsdp'), may hold values from 0.1 to 2
- attn_out: bfloat16 [4, 8192, 1536], P('replica', 'fsdp'), may hold values from -6 to 6
- grad_out: bfloat16 [4, 8192, 1536], P('replica', 'fsdp'), may hold values from -6 to 6
Outputs:
- new_anchor: float32 [1536, 1536], P('fsdp', 'replica')
- new_momentum: float32 [1536, 1536], P('fsdp', 'replica')
- new_local: float32 [4, 1536, 1536], P('replica', 'fsdp')
- new_first: float32 [4, 1536, 1536], P('replica', 'fsdp')
- new_second: float32 [4, 1536, 1536], P('replica', 'fsdp')
- input_grad: bfloat16 [4, 8192, 1536], P('replica', 'fsdp')
All inputs are finite; a program needn't handle non-finite values.
Results may differ from a plain program's by a relative error of at most 0.0049.
Values may be sent and summed in bfloat16 or wider, within the bound.
A program may use at most 128 MiB of HBM per device.

v0:
```python
import functools

import jax
import jax.numpy as jnp
from jax import lax
from jax.experimental import pallas as pl
from jax.experimental.pallas import tpu as pltpu
from jax.sharding import PartitionSpec as P

outer_rate = 0.7
outer_mu = 0.9
inner_rate = 0.005
beta_one = 0.9
beta_two = 0.95
decay_rate = 0.1
epsilon = 1e-08

MESH = pl.DeviceIdType.MESH
f32 = jnp.float32
bf16 = jnp.bfloat16


def adam(anchor_next, first, second, gradient):
    first_next = beta_one * first + (1.0 - beta_one) * gradient
    second_next = beta_two * second + (1.0 - beta_two) * gradient * gradient
    local = anchor_next - inner_rate * (
        first_next / (jnp.sqrt(second_next) + epsilon) + decay_rate * anchor_next
    )
    return local, first_next, second_next


def outer_step(anchor, momentum, summed, groups):
    outer_grad = -summed / groups
    new_momentum = outer_mu * momentum + outer_grad
    new_anchor = anchor - outer_rate * (outer_grad + outer_mu * new_momentum)
    return new_anchor, new_momentum


def plain_shards(anchor, momentum, change, adam_first, adam_second, attn_out, grad_out):
    groups = lax.axis_size("replica")
    summed = lax.psum_scatter(change[0], "replica", scatter_dimension=1, tiled=True)
    new_anchor, new_momentum = outer_step(anchor, momentum, summed, groups)
    anchor_next = lax.all_gather(new_anchor, "replica", axis=1, tiled=True)
    inputs, cotangent = attn_out[0], grad_out[0]
    grad_scale = (inputs.shape[0] * lax.axis_size("fsdp")) ** (-0.5)
    gradient = grad_scale * lax.psum_scatter(
        lax.dot_general(inputs, cotangent, (((0,), (0,)), ((), ())), preferred_element_type=f32),
        "fsdp",
        scatter_dimension=0,
        tiled=True,
    )
    input_grad = lax.dot_general(
        cotangent,
        lax.all_gather(anchor_next.astype(bf16), "fsdp", axis=0, tiled=True),
        (((1,), (1,)), ((), ())),
        preferred_element_type=f32,
    ).astype(bf16)
    local, first, second = adam(anchor_next, adam_first[0], adam_second[0], gradient)
    return new_anchor, new_momentum, local[None], first[None], second[None], input_grad[None]


def kernel(
    depth, groups, scale,
    anchor_hbm, momentum_hbm, change_hbm, attn_hbm, cot_hbm,
    summed_ref, row_ref, grad_ref, back_hbm,
    anchor, momentum, change, attn, cot, flipped,
    part, got, own, psend, ry, zsend, chain, weights, back,
    lead_own, lead_send, lead_chain, lead_out, lead_in,
    local_sem, back_sem, part_s, part_r, py_s, py_r, ch_s, ch_r,
    lz_s, lz_r, ly_s, ly_r,
    az_s, az_r, ay_s, ay_r, ax_s, ax_r, as_s, as_r,
):
    r = lax.axis_index("replica")
    f = lax.axis_index("fsdp")
    x, core = r // 2, r % 2
    z, y = f // 2, f % 2
    rows, width = change.shape
    cols = width // groups
    pair = 2 * rows
    flip_y = {"replica": r, "fsdp": z * 2 + (1 - y)}
    flip_x = {"replica": (1 - x) * 2 + core, "fsdp": f}
    sibling = {"replica": x * 2 + (1 - core), "fsdp": f}

    def along_z(where):
        return {"replica": r, "fsdp": where * 2 + y}

    loads = []
    for i, (src, dst) in enumerate((
        (change_hbm, change), (anchor_hbm, anchor), (momentum_hbm, momentum),
        (attn_hbm, attn), (cot_hbm, cot),
    )):
        loads.append(pltpu.make_async_copy(src, dst, local_sem.at[i]))
        loads[-1].start()

    barrier = pltpu.get_barrier_semaphore()
    for k in range(1, groups):
        pl.semaphore_signal(
            barrier, inc=1, device_id={"replica": (r + k) % groups, "fsdp": f}, device_id_type=MESH
        )
    for k in range(1, depth):
        pl.semaphore_signal(barrier, inc=1, device_id=along_z((z + k) % depth), device_id_type=MESH)
    pl.semaphore_signal(barrier, inc=1, device_id=flip_y, device_id_type=MESH)

    def remote(src, dst, send, recv, device):
        return pltpu.make_async_remote_copy(
            src_ref=src, dst_ref=dst, send_sem=send, recv_sem=recv,
            device_id=device, device_id_type=MESH,
        )

    loads[0].wait()
    for k in range(groups):
        at = pl.multiple_of(((r + k) % groups) * cols, 128)
        part[k] = change[:, pl.ds(at, cols)].astype(bf16)
    pl.semaphore_wait(barrier, groups + depth - 1)
    parts = []
    for k in range(1, groups):
        parts.append(remote(
            part.at[k], got.at[k - 1], part_s.at[k - 1], part_r.at[k - 1],
            {"replica": (r + k) % groups, "fsdp": f},
        ))
        parts[-1].start()

    def block_at(i):
        low = jnp.where(i < depth - 1 - z, depth - 1 - i, i - (depth - 1 - z))
        high = jnp.where(i < z, i, depth - 1 - (i - z))
        return jnp.where(z < depth // 2, low, high)

    lead = lead_own.shape[2]
    half = (width - lead) // 2
    last = depth - 1
    inner = jnp.logical_and(z > 0, z < last)

    def y_copy(i, h):
        there = pl.ds(pl.multiple_of(h * half, 128), half)
        return remote(
            psend.at[i, :, there], ry.at[i, :, there], py_s.at[2 * i + h], py_r.at[2 * i + h],
            flip_y,
        )

    def route(i):
        dest = block_at(i)
        up = dest > z
        return dest + jnp.where(up, 0, depth), along_z(z + jnp.where(up, 1, -1))

    def lead_copy(i):
        slot, device = route(i)
        return remote(
            lead_send.at[i], lead_chain.at[slot], lz_s.at[i], lz_r.at[slot], device
        )

    loads[3].wait()
    loads[4].wait()

    def multiply(i, carry):
        at = pl.multiple_of(block_at(i) * pair, 128)
        flipped[...] = attn[:, pl.ds(at, pair)].T

        def columns(h, carry):
            there = pl.ds(pl.multiple_of(lead + h * half, 128), half)
            product = jnp.dot(flipped[...], cot[:, there], preferred_element_type=f32)
            upper, lower = product[:rows], product[rows:]
            here = pl.ds(pl.multiple_of(h * half, 128), half)
            own[i, :, here] = jnp.where(y == 0, upper, lower)
            psend[i, :, here] = jnp.where(y == 0, lower, upper).astype(bf16)

            @pl.when(i < 2)
            def _():
                y_copy(i, h).start()

            return carry

        lax.fori_loop(0, 2, columns, 0)
        lead_own[i] = jnp.dot(flipped[...], cot[:, :lead], preferred_element_type=f32)

        @pl.when(jnp.logical_and(jnp.logical_not(inner), i < last))
        def _():
            lead_send[i] = lead_own[i].astype(bf16)
            lead_copy(i).start()

        return carry

    lax.fori_loop(0, depth, multiply, 0)

    loads[1].wait()
    loads[2].wait()
    for k in range(1, groups):
        parts[k - 1].wait_recv()
    mine = pl.ds(pl.multiple_of(r * cols, 128), cols)
    total = change[:, mine]
    for k in range(1, groups):
        total = total + got[k - 1].astype(f32)
    summed_ref[...] = total
    weights[f, :, mine] = outer_step(anchor[...], momentum[...], total, groups)[0].astype(bf16)

    def shard(zs, ys, xs, cs):
        at = pl.multiple_of((xs * 2 + cs) * cols, 128)
        return weights.at[zs * 2 + ys, :, pl.ds(at, cols)]

    def forward(kind, sends, recvs, index, where, device):
        ref = shard(*where)
        copy = remote(ref, ref, sends.at[index], recvs.at[index], device)
        copy.start()
        return copy

    def arrived(recvs, sends, index, where):
        ref = shard(*where)
        remote(ref, ref, sends.at[index], recvs.at[index], sibling).wait_recv()

    pending = []
    here = (z, y, x, core)
    for k in range(1, depth):
        pending.append(forward("z", az_s, az_r, k - 1, here, along_z((z + k) % depth)))
    pending.append(forward("y", ay_s, ay_r, 0, here, flip_y))
    pending.append(forward("x", ax_s, ax_r, 0, here, flip_x))
    pending.append(forward("s", as_s, as_r, 0, here, sibling))

    @pl.when(inner)
    def _():
        def pass_on(i, carry):
            slot, _ = route(i)
            copy = lead_copy(i)
            copy.wait_recv()
            lead_send[i] = (lead_own[i] + lead_chain[slot].astype(f32)).astype(bf16)
            copy.start()
            return carry

        lax.fori_loop(0, last, pass_on, 0)

    for k in range(1, depth):
        where = ((z + depth - k) % depth, y, x, core)
        arrived(az_r, az_s, k - 1, where)
        pending.append(forward("y", ay_s, ay_r, k, where, flip_y))
        pending.append(forward("x", ax_s, ax_r, k, where, flip_x))
        pending.append(forward("s", as_s, as_r, k, where, sibling))
    for i in range(2, depth):
        for h in range(2):
            y_copy(i, h).start()

    lines = 16

    def reduce_step(i):
        for h in range(2):
            y_copy(i, h).wait_recv()
        slot, device = route(i)
        copy = remote(zsend.at[i], chain.at[slot], ch_s.at[i], ch_r.at[slot], device)

        @pl.when(inner)
        def _():
            copy.wait_recv()

            def add(j, carry):
                there = pl.ds(pl.multiple_of(j * lines, lines), lines)
                zsend[i, there] = (
                    own[i, there] + ry[i, there].astype(f32) + chain[slot, there].astype(f32)
                ).astype(bf16)
                return carry

            lax.fori_loop(0, rows // lines, add, 0)

        @pl.when(jnp.logical_not(inner))
        def _():
            def add(j, carry):
                there = pl.ds(pl.multiple_of(j * lines, lines), lines)
                zsend[i, there] = (own[i, there] + ry[i, there].astype(f32)).astype(bf16)
                return carry

            lax.fori_loop(0, rows // lines, add, 0)

        copy.start()
        return copy

    chains = [reduce_step(0)]
    for k in range(depth):
        where = ((z + depth - k) % depth, 1 - y, x, core)
        arrived(ay_r, ay_s, k, where)
        pending.append(forward("x", ax_s, ax_r, depth + k, where, flip_x))
        pending.append(forward("s", as_s, as_r, depth + k, where, sibling))
    for slot, follows in ((z, z > 0), (depth + z, z < last)):
        @pl.when(follows)
        def _():
            remote(
                lead_send.at[0], lead_chain.at[slot], lz_s.at[0], lz_r.at[slot], flip_y
            ).wait_recv()
            lead_own[last] += lead_chain[slot].astype(f32)
    lead_out[...] = lead_own[last, pl.ds(pl.multiple_of((1 - y) * rows, 8), rows)].astype(bf16)
    lead_swap = remote(lead_out, lead_in, ly_s.at[0], ly_r.at[0], flip_y)
    lead_swap.start()
    for i in range(1, last):
        chains.append(reduce_step(i))
    for dy in range(2):
        for k in range(depth):
            where = ((z + depth - k) % depth, y + dy - 2 * y * dy, 1 - x, core)
            arrived(ax_r, ax_s, dy * depth + k, where)
            pending.append(forward("s", as_s, as_r, (2 + dy) * depth + k, where, sibling))
    for dx in range(2):
        for dy in range(2):
            for k in range(depth):
                where = (
                    (z + depth - k) % depth, y + dy - 2 * y * dy, x + dx - 2 * x * dx, 1 - core
                )
                arrived(as_r, as_s, (2 * dx + dy) * depth + k, where)
    row_ref[...] = weights[f]

    def back_copy(c):
        there = pl.ds(pl.multiple_of(c * pair, 128), pair)
        return pltpu.make_async_copy(back.at[:, there], back_hbm.at[:, there], back_sem.at[c])

    def back_step(c, carry):
        there = pl.ds(pl.multiple_of(c * pair, 128), pair)
        block = weights[pl.ds(2 * c, 2)].reshape(pair, width)
        back[:, there] = lax.dot_general(
            cot[...], block, (((1,), (1,)), ((), ())), preferred_element_type=f32
        ).astype(bf16)
        back_copy(c).start()
        return carry

    lax.fori_loop(0, depth, back_step, 0)

    lead_swap.wait_recv()
    kept = lead_own[last, pl.ds(pl.multiple_of(y * rows, 8), rows)]
    grad_ref[:, :lead] = (kept + lead_in[...].astype(f32)) * scale
    for h in range(2):
        y_copy(last, h).wait_recv()
    grad_ref[:, lead:] = (own[last] + ry[last].astype(f32)) * scale
    for slot, follows in ((z, z > 0), (depth + z, z < last)):
        @pl.when(follows)
        def _():
            remote(
                zsend.at[0], chain.at[slot], ch_s.at[0], ch_r.at[slot], flip_y
            ).wait_recv()
            grad_ref[:, lead:] += chain[slot].astype(f32) * scale

    for copy in parts + pending + chains + [lead_swap]:
        copy.wait_send()
    for i in range(depth):
        for h in range(2):
            y_copy(i, h).wait_send()
    for i in range(last):
        lead_copy(i).wait_send()
    for c in range(depth):
        back_copy(c).wait()


def lead_columns(width):
    return width // 6 // 128 * 128


def fused_shards(anchor, momentum, change, adam_first, adam_second, attn_out, grad_out):
    groups, devices = lax.axis_size("replica"), lax.axis_size("fsdp")
    depth = devices // 2
    rows, width = change.shape[1:]
    tokens = attn_out.shape[1]
    cols = width // groups
    lead = lead_columns(width)
    rest = width - lead
    scale = (tokens * devices) ** (-0.5)
    dma = pltpu.SemaphoreType.DMA
    vmem = pltpu.VMEM
    any_space = pl.BlockSpec(memory_space=pl.ANY)
    in_vmem = pl.BlockSpec(memory_space=pltpu.VMEM)
    summed, anchor_row, gradient, input_grad = pl.pallas_call(
        functools.partial(kernel, depth, groups, scale),
        out_shape=(
            jax.ShapeDtypeStruct((rows, cols), f32),
            jax.ShapeDtypeStruct((rows, width), bf16),
            jax.ShapeDtypeStruct((rows, width), f32),
            jax.ShapeDtypeStruct((tokens, width), bf16),
        ),
        in_specs=[any_space] * 5,
        out_specs=(in_vmem, in_vmem, in_vmem, any_space),
        scratch_shapes=[
            vmem((rows, cols), f32),
            vmem((rows, cols), f32),
            vmem((rows, width), f32),
            vmem((tokens, width), bf16),
            vmem((tokens, width), bf16),
            vmem((2 * rows, tokens), bf16),
            vmem((groups, rows, cols), bf16),
            vmem((groups - 1, rows, cols), bf16),
            vmem((depth, rows, rest), f32),
            vmem((depth, rows, rest), bf16),
            vmem((depth, rows, rest), bf16),
            vmem((depth, rows, rest), bf16),
            vmem((2 * depth, rows, rest), bf16),
            vmem((devices, rows, width), bf16),
            vmem((tokens, width), bf16),
            vmem((depth, 2 * rows, lead), f32),
            vmem((depth, 2 * rows, lead), bf16),
            vmem((2 * depth, 2 * rows, lead), bf16),
            vmem((rows, lead), bf16),
            vmem((rows, lead), bf16),
            dma((5,)), dma((depth,)),
            dma((groups - 1,)), dma((groups - 1,)),
            dma((2 * depth,)), dma((2 * depth,)),
            dma((depth,)), dma((2 * depth,)),
            dma((depth,)), dma((2 * depth,)), dma((1,)), dma((1,)),
            dma((depth - 1,)), dma((depth - 1,)),
            dma((depth,)), dma((depth,)),
            dma((2 * depth,)), dma((2 * depth,)),
            dma((4 * depth,)), dma((4 * depth,)),
        ],
        compiler_params=pltpu.CompilerParams(
            collective_id=0, has_side_effects=True, vmem_limit_bytes=60 * 2**20
        ),
    )(anchor, momentum, change[0], attn_out[0], grad_out[0])
    new_anchor, new_momentum = outer_step(anchor, momentum, summed, groups)
    local, first, second = adam(anchor_row.astype(f32), adam_first[0], adam_second[0], gradient)
    return new_anchor, new_momentum, local[None], first[None], second[None], input_grad[None]


def shards(*arrays):
    groups, devices = lax.axis_size("replica"), lax.axis_size("fsdp")
    rows, width = arrays[2].shape[1:]
    fits = (
        groups == 4 and devices % 2 == 0 and devices >= 4 and rows % 32 == 0
        and (2 * rows) % 128 == 0 and width % (128 * groups) == 0
        and lead_columns(width) > 0 and (width - lead_columns(width)) % 256 == 0
        and arrays[5].shape[1] * width <= 2**21
    )
    return (fused_shards if fits else plain_shards)(*arrays)


def solution(mesh):
    in_specs = (P("fsdp", "replica"),) * 2 + (P("replica", "fsdp", None),) * 5
    out_specs = (P("fsdp", "replica"),) * 2 + (P("replica", "fsdp", None),) * 4
    return jax.shard_map(shards, mesh=mesh, in_specs=in_specs, out_specs=out_specs, check_vma=False)
```

profile of v0, /device:TPU:0, one launch (start us, length us, event | category | flops | bytes accessed | tf_op | source)
XLA Modules:
  0.0 77.1 jit_solution(11521251748979423458)
XLA Ops:
  0.6 0.0 copy-start.1
  0.6 0.0 copy-start.2
  0.7 0.0 copy-start.4
  0.7 68.6 %shard_map.118 = (f32[192,384]{1,0:T(8,128)}, bf16[192,1536]{1,0:T(8,128)(2,1)}, f32[192,1536]{1,0:T(8,128)}, bf16[1024,1536]{1,0:T(8,128)(2,1)}) custom-call(f32[192,384]{1,0:T(8,128)} %anchor_hbm.1, f32[192,384]{1,0:T(8,128)} %momentum_hbm.1, f32[192,1536]{1,0:T(8,128)} %bitcast.25, bf16[1024,1536]{1,0:T(8,128)(2,1)} %bitcast.23, bf16[1024,1536]{1,0:T(8,128)(2,1)} %bitcast.24), custom_call_target="tpu_custom_call" | custom-call | tf_op jit(solution)/shard_map/pallas_call | solution.py:361
  69.2 0.0 copy-start.3
  69.2 0.0 copy-done.1
  69.3 0.0 copy-done.2
  69.3 1.9 %multiply_subtract_fusion = (f32[192,384]{1,0:T(8,128)}, f32[192,384]{1,0:T(8,128)}) fusion(f32[192,384]{1,0:T(8,128)S(1)} %copy-done.1, f32[192,384]{1,0:T(8,128)} %get-tuple-element.10, f32[192,384]{1,0:T(8,128)S(1)} %copy-done.2), kind=kLoop, calls=%fused_computation.10 | loop fusion | flops 589824 | bytes 1474560 | tf_op jit(solution)/shard_map/sub | solution.py:35
  71.2 0.0 copy-done.4
  71.2 0.0 copy-done.3
  71.2 0.0 copy-start
  71.2 4.2 %fusion.5 = (f32[1,192,1536]{2,1,0:T(8,128)}, f32[1,192,1536]{2,1,0:T(8,128)}, f32[1,192,1536]{2,1,0:T(8,128)}) fusion(f32[192,1536]{1,0:T(8,128)} %get-tuple-element.12, f32[1,192,1536]{2,1,0:T(8,128)S(1)} %copy-done.3, f32[1,192,1536]{2,1,0:T(8,128)S(1)} %copy-done.4, bf16[192,1536]{1,0:T(8,128)(2,1)} %get-tuple-element.11), kind=kLoop, calls=%fused_computation.9 | loop fusion | flops 4128768 | bytes 7667712 | tf_op jit(solution)/shard_map/broadcast_in_dim | solution.py:408
  75.4 0.0 copy-done
  75.4 1.7 %copy.14 = bf16[1,1024,1536]{2,1,0:T(8,128)(2,1)} copy(bf16[1,1024,1536]{2,1,0:T(8,128)(2,1)S(1)} %bitcast.22) | data formatting | bytes 6291456
Async XLA Ops:
  0.6 68.6 %copy-start.1 = (f32[192,384]{1,0:T(8,128)S(1)}, f32[192,384]{1,0:T(8,128)}, u32[]{:S(2)}) copy-start(f32[192,384]{1,0:T(8,128)} %anchor_hbm.1) | copy-start | bytes 884740
  0.6 68.6 %copy-start.2 = (f32[192,384]{1,0:T(8,128)S(1)}, f32[192,384]{1,0:T(8,128)}, u32[]{:S(2)}) copy-start(f32[192,384]{1,0:T(8,128)} %momentum_hbm.1) | copy-start | bytes 884740
  0.7 70.6 %copy-start.4 = (f32[1,192,1536]{2,1,0:T(8,128)S(1)}, f32[1,192,1536]{2,1,0:T(8,128)}, u32[]{:S(2)}) copy-start(f32[1,192,1536]{2,1,0:T(8,128)} %param.10) | copy-start | bytes 3538948
  69.2 2.0 %copy-start.3 = (f32[1,192,1536]{2,1,0:T(8,128)S(1)}, f32[1,192,1536]{2,1,0:T(8,128)}, u32[]{:S(2)}) copy-start(f32[1,192,1536]{2,1,0:T(8,128)} %param.11) | copy-start | bytes 3538948
  71.2 4.2 %copy-start = (bf16[1024,1536]{1,0:T(8,128)(2,1)S(1)}, bf16[1024,1536]{1,0:T(8,128)(2,1)}, u32[]{:S(2)}) copy-start(bf16[1024,1536]{1,0:T(8,128)(2,1)} %get-tuple-element.13) | copy-start | bytes 9437188
where the time goes:
time: 78.3 us; the launch traced here: 77.1 us
  Pallas kernels  68.6 us (88%)
  other arithmetic  6.14 us (8%)
  local copies, waits for them, and re-layouts  1.69 us (2%)
    pallas_call x1, Pallas kernels, fused_shards(): pl.pallas_call(functools.partial(kernel, depth, groups, scale), out_shape...  68.6 us
    broadcast_in_dim x1, other arithmetic, fused_shards(): second[None]  4.2 us
    sub x1, other arithmetic, outer_step(): new_anchor = anchor - outer_rate * (outer_grad + outer_mu * new_momentum)  1.94 us
    unnamed x11, local copies, waits for them, and re-layouts  1.69 us

commit v1 on v0

v1 whole, which is shorter than its diff:
```python
import functools

import jax
import jax.numpy as jnp
from jax import lax
from jax.experimental import pallas as pl
from jax.experimental.pallas import tpu as pltpu
from jax.sharding import PartitionSpec as P

outer_rate = 0.7
outer_mu = 0.9
inner_rate = 0.005
beta_one = 0.9
beta_two = 0.95
decay_rate = 0.1
epsilon = 1e-08

MESH = pl.DeviceIdType.MESH
f32 = jnp.float32
bf16 = jnp.bfloat16


def adam(anchor_next, first, second, gradient):
    first_next = beta_one * first + (1.0 - beta_one) * gradient
    second_next = beta_two * second + (1.0 - beta_two) * gradient * gradient
    local = anchor_next - inner_rate * (
        first_next / (jnp.sqrt(second_next) + epsilon) + decay_rate * anchor_next
    )
    return local, first_next, second_next


def outer_step(anchor, momentum, summed, groups):
    outer_grad = -summed / groups
    new_momentum = outer_mu * momentum + outer_grad
    new_anchor = anchor - outer_rate * (outer_grad + outer_mu * new_momentum)
    return new_anchor, new_momentum


def plain_shards(anchor, momentum, change, adam_first, adam_second, attn_out, grad_out):
    groups = lax.axis_size("replica")
    summed = lax.psum_scatter(change[0], "replica", scatter_dimension=1, tiled=True)
    new_anchor, new_momentum = outer_step(anchor, momentum, summed, groups)
    anchor_next = lax.all_gather(new_anchor, "replica", axis=1, tiled=True)
    inputs, cotangent = attn_out[0], grad_out[0]
    grad_scale = (inputs.shape[0] * lax.axis_size("fsdp")) ** (-0.5)
    gradient = grad_scale * lax.psum_scatter(
        lax.dot_general(inputs, cotangent, (((0,), (0,)), ((), ())), preferred_element_type=f32),
        "fsdp",
        scatter_dimension=0,
        tiled=True,
    )
    input_grad = lax.dot_general(
        cotangent,
        lax.all_gather(anchor_next.astype(bf16), "fsdp", axis=0, tiled=True),
        (((1,), (1,)), ((), ())),
        preferred_element_type=f32,
    ).astype(bf16)
    local, first, second = adam(anchor_next, adam_first[0], adam_second[0], gradient)
    return new_anchor, new_momentum, local[None], first[None], second[None], input_grad[None]


INNER_STEPS = (
    "own", "L0", "ab0", "L1", "aa0", "y11", "y21", "ao1", "y31", "L2", "y10", "aa1", "ac0", "xo1", "S01",
    "xa0", "ab1", "ac1", "S00", "xa1", "y30", "S21", "xb0", "S11", "xc0", "CL", "S20", "xb1", "xc1", "S10",
    "Ma", "Mb", "Mc", "xo0", "FL", "Mo", "F1", "F0",
)
OUTER_STEPS = (
    "own", "S01", "ab0", "xo0", "ac0", "S00", "C0", "S11", "ab1", "S10", "L2", "xb0", "ao1", "ad0", "S21",
    "ac1", "ad1", "xc0", "xo1", "xd0", "xc1", "xb1", "CL", "S20", "Mo", "xd1", "Mc", "Mb", "Md", "FL", "F1",
    "F0",
)
ROUTES = {
    True: {"o0": "bayxs", "a0": "ybxs", "o1": "abxs", "a1": "abxs"},
    False: {"o0": "bxs"},
}
LONE = {True: "axs", False: "xs"}


def kernel(
    depth, groups, scale, lead, cuts,
    anchor_hbm, momentum_hbm, change_hbm, attn_hbm, cot_hbm,
    summed_ref, row_ref, grad_ref, back,
    anchor, momentum, change, attn, cot, flipped,
    part, got, own, other, psend, ry, zsend, chain, weights,
    lead_own, lead_send, lead_chain, lead_out, lead_in,
    local_sem, part_s, part_r, py_s, py_r, ch_s, ch_r,
    lz_s, lz_r, ly_s, ly_r, ag_s, ag_r,
):
    r = lax.axis_index("replica")
    f = lax.axis_index("fsdp")
    x, core = r // 2, r % 2
    z, y = f // 2, f % 2
    over_x, over_y = 1 - x, 1 - y
    rows, width = change.shape
    cols = width // groups
    pair = 2 * rows
    last = depth - 1
    pieces = len(cuts)
    inner = jnp.logical_and(z > 0, z < last)
    low = z < depth // 2
    inward = z + jnp.where(low, 1, -1)
    outward = z - jnp.where(low, 1, -1)
    places = {
        True: {"o": z, "a": outward, "b": inward, "c": last - outward},
        False: {"o": z, "b": inward, "c": last - inward, "d": last - z},
    }
    flip_y = {"replica": r, "fsdp": z * 2 + over_y}
    sibling = {"replica": x * 2 + (1 - core), "fsdp": f}
    to_inward = {"replica": r, "fsdp": inward * 2 + y}
    to_outward = {"replica": r, "fsdp": outward * 2 + y}
    links = {
        "a": to_outward, "b": to_inward, "y": flip_y, "s": sibling,
        "x": {"replica": over_x * 2 + core, "fsdp": f},
    }

    loads = []
    for i, (src, dst) in enumerate((
        (change_hbm, change), (attn_hbm, attn), (cot_hbm, cot),
        (anchor_hbm, anchor), (momentum_hbm, momentum),
    )):
        loads.append(pltpu.make_async_copy(src, dst, local_sem.at[i]))
        loads[-1].start()

    barrier = pltpu.get_barrier_semaphore()
    for k in range(1, groups):
        pl.semaphore_signal(
            barrier, inc=1, device_id={"replica": (r + k) % groups, "fsdp": f}, device_id_type=MESH
        )
    pl.semaphore_signal(barrier, inc=1, device_id=flip_y, device_id_type=MESH)
    pl.semaphore_signal(barrier, inc=1, device_id=to_inward, device_id_type=MESH)

    @pl.when(inner)
    def _():
        pl.semaphore_signal(barrier, inc=1, device_id=to_outward, device_id_type=MESH)

    def remote(src, dst, send, recv, device):
        return pltpu.make_async_remote_copy(
            src_ref=src, dst_ref=dst, send_sem=send, recv_sem=recv,
            device_id=device, device_id_type=MESH,
        )

    loads[0].wait()
    for k in range(1, groups):
        at = pl.multiple_of(((r + k) % groups) * cols, 128)
        part[k] = change[:, pl.ds(at, cols)].astype(bf16)
    pl.semaphore_wait(barrier, groups + 1 + jnp.where(inner, 1, 0))
    parts = []
    for k in range(1, groups):
        parts.append(remote(
            part.at[k], got.at[k - 1], part_s.at[k - 1], part_r.at[k - 1],
            {"replica": (r + k) % groups, "fsdp": f},
        ))
        parts[-1].start()

    def block_at(i):
        lower = jnp.where(i < last - z, last - i, i - (last - z))
        upper = jnp.where(i < z, i, last - (i - z))
        return jnp.where(low, lower, upper)

    lines = 16

    def by_rows(body, count):
        def step(j, carry):
            body(pl.ds(pl.multiple_of(j * lines, lines), lines))
            return carry

        lax.fori_loop(0, count // lines, step, 0)

    def piece(h):
        return pl.ds(*cuts[h])

    def y_copy(i, h):
        return remote(
            psend.at[i, :, piece(h)], ry.at[i, :, piece(h)],
            py_s.at[pieces * i + h], py_r.at[pieces * i + h], flip_y,
        )

    def route(inside, i):
        if not inside:
            return i, to_inward
        return (depth - 1 + i, to_inward) if i < 2 else (depth - 1, to_outward)

    def lead_copy(inside, i):
        slot, device = route(inside, i)
        return remote(lead_send.at[i], lead_chain.at[slot], lz_s.at[i], lz_r.at[slot], device)

    def z_copy(inside, i, h):
        slot, device = route(inside, i)
        return remote(
            zsend.at[i, :, piece(h)], chain.at[slot, :, piece(h)],
            ch_s.at[pieces * i + h], ch_r.at[pieces * slot + h], device,
        )

    def extra_copy(h):
        return remote(
            psend.at[2, :, piece(h)], chain.at[depth, :, piece(h)],
            ch_s.at[pieces * last + h], ch_r.at[pieces * depth + h], to_outward,
        )

    def lead_arrived(slot):
        remote(
            lead_send.at[0], lead_chain.at[slot], lz_s.at[0], lz_r.at[slot], flip_y
        ).wait_recv()

    def z_arrived(slot, h):
        remote(
            zsend.at[0, :, piece(h)], chain.at[slot, :, piece(h)],
            ch_s.at[h], ch_r.at[pieces * slot + h], flip_y,
        ).wait_recv()

    sends = {True: [], False: []}

    def start(inside, make):
        make().start()
        sends[inside].append(make)

    loads[1].wait()
    loads[2].wait()

    def multiply(i, carry):
        at = pl.multiple_of(block_at(i) * pair, 128)
        flipped[...] = attn[:, pl.ds(at, pair)].T
        for h in range(pieces):
            product = jnp.dot(flipped[...], cot[:, piece(h)], preferred_element_type=f32)
            upper, lower = product[:rows], product[rows:]
            own[i, :, piece(h)] = jnp.where(y == 0, upper, lower)
            across = jnp.where(y == 0, lower, upper)
            psend[i, :, piece(h)] = across.astype(bf16)

            @pl.when(i == last)
            def _():
                other[:, piece(h)] = across

            early = jnp.where(inner, i == 0, i < last if h == 0 else i <= last)

            @pl.when(early)
            def _():
                y_copy(i, h).start()

            if h == 0:
                @pl.when(jnp.logical_and(inner, i == 2))
                def _():
                    extra_copy(h).start()

        lead_own[i] = jnp.dot(flipped[...], cot[:, :lead], preferred_element_type=f32)

        @pl.when(jnp.logical_and(jnp.logical_not(inner), i < last))
        def _():
            lead_send[i] = lead_own[i].astype(bf16)

            @pl.when(i < 2)
            def _():
                lead_copy(False, i).start()

        return carry

    lax.fori_loop(0, depth, multiply, 0)
    for h in range(pieces):
        sends[True].append(functools.partial(y_copy, 0, h))
        for i in range(depth if h else last):
            sends[False].append(functools.partial(y_copy, i, h))
    sends[True].append(functools.partial(extra_copy, 0))
    for i in range(2):
        sends[False].append(functools.partial(lead_copy, False, i))

    loads[3].wait()
    loads[4].wait()
    for k in range(1, groups):
        parts[k - 1].wait_recv()
    mine = pl.ds(pl.multiple_of(r * cols, 128), cols)
    total = change[:, mine]
    for k in range(1, groups):
        total = total + got[k - 1].astype(f32)
    summed_ref[...] = total
    weights[f, :, mine] = outer_step(anchor[...], momentum[...], total, groups)[0].astype(bf16)

    def shard_copy(where, index, device):
        zs, ys, xs, cs = where
        at = pl.multiple_of((xs * 2 + cs) * cols, 128)
        ref = weights.at[zs * 2 + ys, :, pl.ds(at, cols)]
        return remote(
            ref, ref, ag_s.at[index], ag_r.at[((zs * 2 + ys) * 2 + xs) * 2 + cs], device
        )

    def arrived(where):
        shard_copy(where, 0, sibling).wait_recv()

    used = {True: 0, False: 0}

    def spread(inside, where, names):
        for name in names:
            start(inside, functools.partial(shard_copy, where, used[inside], links[name]))
            used[inside] += 1

    def lead_step(inside, i):
        if inside:
            slot = i if i < 2 else depth - 1
            lead_arrived(slot)

            def add(there):
                lead_send[i, there] = (
                    lead_own[i, there] + lead_chain[slot, there].astype(f32)
                ).astype(bf16)

            by_rows(add, pair)
        start(inside, functools.partial(lead_copy, inside, i))

    def chain_step(inside, i, h):
        crossed = not inside or i < 2 or h > 0
        slot = i if i < 2 else depth - 1
        if crossed:
            y_copy(i, h).wait_recv()
        if inside:
            z_arrived(slot, h)

        def add(there):
            value = own[i, there, piece(h)]
            if crossed:
                value = value + ry[i, there, piece(h)].astype(f32)
            if inside:
                value = value + chain[slot, there, piece(h)].astype(f32)
            zsend[i, there, piece(h)] = value.astype(bf16)

        by_rows(add, rows)
        start(inside, functools.partial(z_copy, inside, i, h))

    def cross_step(h):
        z_arrived(depth, h)

        def add(there):
            psend[last, there, piece(h)] = (
                other[there, piece(h)] + chain[depth, there, piece(h)].astype(f32)
            ).astype(bf16)

        by_rows(add, rows)
        start(False, functools.partial(y_copy, last, h))

    ends = {True: (2, depth), False: (depth - 1,)}

    def lead_swap():
        return remote(lead_out, lead_in, ly_s.at[0], ly_r.at[0], flip_y)

    away = pl.multiple_of((1 - y) * rows, 8)
    home = pl.multiple_of(y * rows, 8)

    def cross_lead(inside):
        for slot in ends[inside]:
            lead_arrived(slot)
        value = lead_own[last, pl.ds(away, rows)]
        for slot in ends[inside]:
            value = value + lead_chain[slot, pl.ds(away, rows)].astype(f32)
        lead_out[...] = value.astype(bf16)
        start(inside, lead_swap)

    def finish_lead(inside):
        lead_swap().wait_recv()
        value = lead_own[last, pl.ds(home, rows)] + lead_in[...].astype(f32)
        for slot in ends[inside]:
            value = value + lead_chain[slot, pl.ds(home, rows)].astype(f32)
        grad_ref[:, :lead] = value * scale

    def finish(inside, h):
        y_copy(last, h).wait_recv()
        for slot in ends[inside]:
            z_arrived(slot, h)

        def add(there):
            value = own[last, there, piece(h)] + ry[last, there, piece(h)].astype(f32)
            for slot in ends[inside]:
                value = value + chain[slot, there, piece(h)].astype(f32)
            grad_ref[there, piece(h)] = value * scale

        by_rows(add, rows)

    def take(inside, step):
        kind, spot = step[0], step[1:]
        if step == "own":
            spread(inside, (z, y, x, core), ROUTES[inside]["o0"])
        elif kind in "ax":
            zs, ys = places[inside][spot[0]], y if spot[1] == "0" else over_y
            if kind == "a":
                where = (zs, ys, x, core)
                arrived(where)
                spread(inside, where, ROUTES[inside].get(spot, LONE[inside]))
            else:
                where = (zs, ys, over_x, core)
                arrived(where)
                spread(inside, where, "s")
        elif kind == "L":
            lead_step(inside, int(spot))
        elif kind == "S":
            chain_step(inside, int(spot[0]), int(spot[1]))
        elif kind == "y":
            start(inside, functools.partial(y_copy, int(spot[0]), int(spot[1])))
        elif step == "CL":
            cross_lead(inside)
        elif kind == "C":
            cross_step(int(spot))
        elif step == "FL":
            finish_lead(inside)
        elif kind == "F":
            finish(inside, int(spot))

    runs, outs = {}, {}
    for inside, steps in ((True, INNER_STEPS), (False, OUTER_STEPS)):
        runs[inside], outs[inside] = [[]], []
        for step in steps:
            if step[0] == "M":
                outs[inside].append(places[inside][step[1]])
                runs[inside].append([])
            else:
                runs[inside][-1].append(step)

    for k in range(depth + 1):
        for inside in (True, False):
            @pl.when(inner if inside else jnp.logical_not(inner))
            def _():
                for step in runs[inside][k]:
                    take(inside, step)

        if k < depth:
            zs = jnp.where(inner, outs[True][k], outs[False][k])
            for ys in range(2):
                for xs in range(2):
                    arrived((zs, ys, xs, 1 - core))
            there = pl.ds(pl.multiple_of(zs * pair, 128), pair)
            block = weights[pl.ds(2 * zs, 2)].reshape(pair, width)
            back[:, there] = lax.dot_general(
                cot[...], block, (((1,), (1,)), ((), ())), preferred_element_type=f32
            ).astype(bf16)

    row_ref[...] = weights[f]
    for copy in parts:
        copy.wait_send()
    for inside in (True, False):
        @pl.when(inner if inside else jnp.logical_not(inner))
        def _():
            for make in sends[inside]:
                make().wait_send()


def finish_kernel(
    groups, lines,
    anchor, momentum, summed, row, first, second, gradient, back,
    anchor_hbm, momentum_hbm, local_hbm, first_hbm, second_hbm, back_hbm,
    anchor_out, momentum_out, local_out, first_out, second_out, sems,
):
    copies = []

    def put(src, dst):
        copies.append(pltpu.make_async_copy(src, dst, sems.at[len(copies)]))
        copies[-1].start()

    put(back, back_hbm)
    for k in range(row.shape[0] // lines):
        there = pl.ds(k * lines, lines)
        local, first_next, second_next = adam(
            row[there].astype(f32), first[there], second[there], gradient[there]
        )
        first_out[there] = first_next
        put(first_out.at[there], first_hbm.at[there])
        second_out[there] = second_next
        put(second_out.at[there], second_hbm.at[there])
        local_out[there] = local
        put(local_out.at[there], local_hbm.at[there])
    new_anchor, new_momentum = outer_step(anchor[...], momentum[...], summed[...], groups)
    anchor_out[...] = new_anchor
    put(anchor_out, anchor_hbm)
    momentum_out[...] = new_momentum
    put(momentum_out, momentum_hbm)
    for copy in copies:
        copy.wait()


def plan(width):
    lead = width // 6 // 128 * 128
    half = (width - lead) // 256 * 128
    return lead, ((lead, half), (lead + half, width - lead - half))


def fused_shards(anchor, momentum, change, adam_first, adam_second, attn_out, grad_out):
    groups, devices = lax.axis_size("replica"), lax.axis_size("fsdp")
    depth = devices // 2
    rows, width = change.shape[1:]
    tokens = attn_out.shape[1]
    cols = width // groups
    lead, cuts = plan(width)
    rest = width - lead
    pieces = len(cuts)
    scale = (tokens * devices) ** (-0.5)
    dma = pltpu.SemaphoreType.DMA
    vmem = pltpu.VMEM
    in_hbm = pl.BlockSpec(memory_space=pltpu.HBM)
    in_vmem = pl.BlockSpec(memory_space=pltpu.VMEM)
    summed, anchor_row, gradient, input_grad = pl.pallas_call(
        functools.partial(kernel, depth, groups, scale, lead, cuts),
        out_shape=(
            jax.ShapeDtypeStruct((rows, cols), f32),
            jax.ShapeDtypeStruct((rows, width), bf16),
            jax.ShapeDtypeStruct((rows, width), f32),
            jax.ShapeDtypeStruct((tokens, width), bf16),
        ),
        in_specs=[in_hbm] * 5,
        out_specs=(in_vmem,) * 4,
        scratch_shapes=[
            vmem((rows, cols), f32),
            vmem((rows, cols), f32),
            vmem((rows, width), f32),
            vmem((tokens, width), bf16),
            vmem((tokens, width), bf16),
            vmem((2 * rows, tokens), bf16),
            vmem((groups, rows, cols), bf16),
            vmem((groups - 1, rows, cols), bf16),
            vmem((depth, rows, width), f32),
            vmem((rows, width), f32),
            vmem((depth, rows, width), bf16),
            vmem((depth, rows, width), bf16),
            vmem((depth - 1, rows, width), bf16),
            vmem((depth + 1, rows, width), bf16),
            vmem((devices, rows, width), bf16),
            vmem((depth, 2 * rows, lead), f32),
            vmem((depth - 1, 2 * rows, lead), bf16),
            vmem((depth + 1, 2 * rows, lead), bf16),
            vmem((rows, lead), bf16),
            vmem((rows, lead), bf16),
            dma((5,)),
            dma((groups - 1,)), dma((groups - 1,)),
            dma((depth * pieces,)), dma((depth * pieces,)),
            dma((depth * pieces,)), dma(((depth + 1) * pieces,)),
            dma((depth - 1,)), dma((depth + 1,)), dma((1,)), dma((1,)),
            dma((5 * devices,)), dma((groups * devices,)),
        ],
        compiler_params=pltpu.CompilerParams(
            collective_id=0, has_side_effects=True, vmem_limit_bytes=38 * 2**20
        ),
    )(*(
        pltpu.with_memory_space_constraint(array, pltpu.HBM)
        for array in (anchor, momentum, change[0], attn_out[0], grad_out[0])
    ))
    lines = rows // 4
    block = jax.ShapeDtypeStruct((rows, width), f32)
    quarter = jax.ShapeDtypeStruct((rows, cols), f32)
    outs = pl.pallas_call(
        functools.partial(finish_kernel, groups, lines),
        out_shape=(
            quarter, quarter, block, block, block, jax.ShapeDtypeStruct((tokens, width), bf16),
        ),
        in_specs=[in_vmem] * 8,
        out_specs=(in_hbm,) * 6,
        scratch_shapes=[
            vmem((rows, cols), f32), vmem((rows, cols), f32),
            vmem((rows, width), f32), vmem((rows, width), f32), vmem((rows, width), f32),
            dma((3 * (rows // lines) + 3,)),
        ],
        compiler_params=pltpu.CompilerParams(vmem_limit_bytes=12 * 2**20),
    )(anchor, momentum, summed, anchor_row, adam_first[0], adam_second[0], gradient, input_grad)
    return (*outs[:2], *(out[None] for out in outs[2:]))


def shards(*arrays):
    groups, devices = lax.axis_size("replica"), lax.axis_size("fsdp")
    rows, width = arrays[2].shape[1:]
    fits = (
        groups == 4 and devices == 8 and rows % 32 == 0
        and (2 * rows) % 128 == 0 and width % (128 * groups) == 0
        and plan(width)[0] > 0
        and arrays[5].shape[1] * width <= 2**21
    )
    return (fused_shards if fits else plain_shards)(*arrays)


def solution(mesh):
    in_specs = (P("fsdp", "replica"),) * 2 + (P("replica", "fsdp", None),) * 5
    out_specs = (P("fsdp", "replica"),) * 2 + (P("replica", "fsdp", None),) * 4
    return jax.shard_map(shards, mesh=mesh, in_specs=in_specs, out_specs=out_specs, check_vma=False)
```

time: 78.3 us -> 62.9 us (0.80)
  the two profiles are of different devices: /device:TPU:0 before, /device:TPU:14 now
where the time goes in v1:
time: 62.9 us; the launch traced here: 62.8 us
  Pallas kernels  62.1 us (99%)
  between operations  0.71 us (1%)
    pallas_call x1, Pallas kernels, fused_shards(): pl.pallas_call(functools.partial(kernel, depth, groups, scale, lead, cuts...  59 us
    pallas_call x1, Pallas kernels, fused_shards(): pl.pallas_call(functools.partial(finish_kernel, groups, lines), out_shape...  3.07 us

profile of v1, /device:TPU:14, one launch (start us, length us, event | category | flops | bytes accessed | tf_op | source)
XLA Modules:
  0.0 62.8 jit_solution(3756481328222032552)
XLA Ops:
  0.6 0.0 copy-start
  0.6 0.0 copy-start.1
  0.7 0.0 copy-start.2
  0.7 0.0 copy-start.3
  0.7 59.0 %shard_map.118 = (f32[192,384]{1,0:T(8,128)S(1)}, bf16[192,1536]{1,0:T(8,128)(2,1)S(1)}, f32[192,1536]{1,0:T(8,128)S(1)}, bf16[1024,1536]{1,0:T(8,128)(2,1)S(1)}) custom-call(f32[192,384]{1,0:T(8,128)} %anchor.1, f32[192,384]{1,0:T(8,128)} %momentum.1, f32[192,1536]{1,0:T(8,128)} %bitcast.13, bf16[1024,1536]{1,0:T(8,128)(2,1)} %bitcast.11, ...), custom_call_target="tpu_custom_call" | custom-call | tf_op jit(solution)/shard_map/pallas_call | solution.py:495
  59.7 0.0 copy-done
  59.7 0.0 copy-done.1
  59.7 0.0 copy-done.2
  59.7 0.0 copy-done.3
  59.7 3.1 %shard_map.119 = (f32[192,384]{1,0:T(8,128)}, f32[192,384]{1,0:T(8,128)}, f32[192,1536]{1,0:T(8,128)}, f32[192,1536]{1,0:T(8,128)}, f32[192,1536]{1,0:T(8,128)}, /*index=5*/bf16[1024,1536]{1,0:T(8,128)(2,1)}) custom-call(f32[192,384]{1,0:T(8,128)S(1)} %copy-done, f32[192,384]{1,0:T(8,128)S(1)} %copy-done.1, f32[192,384]{1,0:T(8,128)S(1)} %get-tuple-element.16.summed, ...), custom_call_target="tpu_custom_call" | custom-call | tf_op jit(solution)/shard_map/pallas_call | solution.py:543
Async XLA Ops:
  0.6 59.1 %copy-start = (f32[192,384]{1,0:T(8,128)S(1)}, f32[192,384]{1,0:T(8,128)}, u32[]{:S(2)}) copy-start(f32[192,384]{1,0:T(8,128)} %anchor.1) | copy-start | bytes 884740
  0.6 59.1 %copy-start.1 = (f32[192,384]{1,0:T(8,128)S(1)}, f32[192,384]{1,0:T(8,128)}, u32[]{:S(2)}) copy-start(f32[192,384]{1,0:T(8,128)} %momentum.1) | copy-start | bytes 884740
  0.7 59.1 %copy-start.2 = (f32[1,192,1536]{2,1,0:T(8,128)S(1)}, f32[1,192,1536]{2,1,0:T(8,128)}, u32[]{:S(2)}) copy-start(f32[1,192,1536]{2,1,0:T(8,128)} %param.10) | copy-start | bytes 3538948
  0.7 59.1 %copy-start.3 = (f32[1,192,1536]{2,1,0:T(8,128)S(1)}, f32[1,192,1536]{2,1,0:T(8,128)}, u32[]{:S(2)}) copy-start(f32[1,192,1536]{2,1,0:T(8,128)} %param.11) | copy-start | bytes 3538948

commit v2 on v1

--- a/solution.py
+++ b/solution.py
@@ -60,24 +60,26 @@
 
 
 INNER_STEPS = (
-    "own", "L0", "ab0", "L1", "aa0", "y11", "y21", "ao1", "y31", "L2", "y10", "aa1", "ac0", "xo1", "S01",
-    "xa0", "ab1", "ac1", "S00", "xa1", "y30", "S21", "xb0", "S11", "xc0", "CL", "S20", "xb1", "xc1", "S10",
-    "Ma", "Mb", "Mc", "xo0", "FL", "Mo", "F1", "F0",
+    "B00", "y00", "B0L", "B01", "B10", "B1L", "B11", "B20", "y01", "E0", "B2L", "B21", "B30", "L0", "B3L",
+    "B31", "W", "own", "y11", "L2", "aa0", "ao1", "ac0", "L1", "ab0", "xo0", "S00", "y10", "ab1", "S01",
+    "aa1", "xc0", "xa0", "ac1", "xo1", "y21", "xb0", "y31", "Mo", "S11", "xa1", "S20", "xb1", "y30", "S10",
+    "CL", "Mb", "S21", "xc1", "Ma", "Mc", "F0", "F1", "FL",
 )
 OUTER_STEPS = (
-    "own", "S01", "ab0", "xo0", "ac0", "S00", "C0", "S11", "ab1", "S10", "L2", "xb0", "ao1", "ad0", "S21",
-    "ac1", "ad1", "xc0", "xo1", "xd0", "xc1", "xb1", "CL", "S20", "Mo", "xd1", "Mc", "Mb", "Md", "FL", "F1",
-    "F0",
+    "B00", "y00", "B0L", "L0", "B01", "B10", "B1L", "B11", "B20", "L1", "B2L", "y01", "B21", "B30", "B3L",
+    "B31", "W", "own", "yL", "S00", "y11", "y10", "y20", "S01", "ab0", "xo0", "L2", "ab1", "S11", "ad0",
+    "CL", "S10", "y21", "ac0", "xb1", "S20", "xb0", "ac1", "C0", "FL", "ao1", "Mb", "xc1", "S21", "ad1",
+    "y31", "xc0", "xd0", "xo1", "Mc", "xd1", "Mo", "F0", "Md", "F1",
 )
 ROUTES = {
-    True: {"o0": "bayxs", "a0": "ybxs", "o1": "abxs", "a1": "abxs"},
+    True: {"o0": "bayxs", "a0": "ybxs", "o1": "abxs", "a1": "axs", "c0": "yaxs"},
     False: {"o0": "bxs"},
 }
 LONE = {True: "axs", False: "xs"}
 
 
 def kernel(
-    depth, groups, scale, lead, cuts,
+    depth, groups, scale, lead, cuts, extras,
     anchor_hbm, momentum_hbm, change_hbm, attn_hbm, cot_hbm,
     summed_ref, row_ref, grad_ref, back,
     anchor, momentum, change, attn, cot, flipped,
@@ -113,13 +115,32 @@
         "x": {"replica": over_x * 2 + core, "fsdp": f},
     }
 
+    def block_at(i):
+        lower = jnp.where(i < last - z, last - i, i - (last - z))
+        upper = jnp.where(i < z, i, last - (i - z))
+        return jnp.where(low, lower, upper)
+
+    def block_columns(i):
+        return pl.ds(pl.multiple_of(block_at(i) * pair, 128), pair)
+
+    def piece(h):
+        return pl.ds(*cuts[h]) if h < pieces else pl.ds(0, lead)
+
     loads = []
-    for i, (src, dst) in enumerate((
-        (change_hbm, change), (attn_hbm, attn), (cot_hbm, cot),
-        (anchor_hbm, anchor), (momentum_hbm, momentum),
-    )):
-        loads.append(pltpu.make_async_copy(src, dst, local_sem.at[i]))
+
+    def load(src, dst):
+        loads.append(pltpu.make_async_copy(src, dst, local_sem.at[len(loads)]))
         loads[-1].start()
+        return loads[-1]
+
+    attn_in = [load(attn_hbm.at[:, block_columns(0)], attn.at[0])]
+    cot_in = {0: load(cot_hbm.at[:, piece(0)], cot.at[:, piece(0)])}
+    change_in = load(change_hbm, change)
+    for h in (pieces, *range(1, pieces)):
+        cot_in[h] = load(cot_hbm.at[:, piece(h)], cot.at[:, piece(h)])
+    for i in range(1, depth):
+        attn_in.append(load(attn_hbm.at[:, block_columns(i)], attn.at[i]))
+    outer_in = (load(anchor_hbm, anchor), load(momentum_hbm, momentum))
 
     barrier = pltpu.get_barrier_semaphore()
     for k in range(1, groups):
@@ -139,7 +160,7 @@
             device_id=device, device_id_type=MESH,
         )
 
-    loads[0].wait()
+    change_in.wait()
     for k in range(1, groups):
         at = pl.multiple_of(((r + k) % groups) * cols, 128)
         part[k] = change[:, pl.ds(at, cols)].astype(bf16)
@@ -152,11 +173,6 @@
         ))
         parts[-1].start()
 
-    def block_at(i):
-        lower = jnp.where(i < last - z, last - i, i - (last - z))
-        upper = jnp.where(i < z, i, last - (i - z))
-        return jnp.where(low, lower, upper)
-
     lines = 16
 
     def by_rows(body, count):
@@ -166,13 +182,10 @@
 
         lax.fori_loop(0, count // lines, step, 0)
 
-    def piece(h):
-        return pl.ds(*cuts[h])
-
     def y_copy(i, h):
         return remote(
             psend.at[i, :, piece(h)], ry.at[i, :, piece(h)],
-            py_s.at[pieces * i + h], py_r.at[pieces * i + h], flip_y,
+            py_s.at[(pieces + 1) * i + h], py_r.at[(pieces + 1) * i + h], flip_y,
         )
 
     def route(inside, i):
@@ -180,9 +193,16 @@
             return i, to_inward
         return (depth - 1 + i, to_inward) if i < 2 else (depth - 1, to_outward)
 
+    away = pl.multiple_of((1 - y) * rows, 16)
+    home = pl.multiple_of(y * rows, 16)
+
+    def lead_rows(ref, slot):
+        return ref.at[slot, pl.ds(home, rows)] if slot == 2 else ref.at[slot]
+
     def lead_copy(inside, i):
         slot, device = route(inside, i)
-        return remote(lead_send.at[i], lead_chain.at[slot], lz_s.at[i], lz_r.at[slot], device)
+        src = lead_send.at[i] if inside else lead_rows(lead_send, i)
+        return remote(src, lead_rows(lead_chain, slot), lz_s.at[i], lz_r.at[slot], device)
 
     def z_copy(inside, i, h):
         slot, device = route(inside, i)
@@ -198,9 +218,8 @@
         )
 
     def lead_arrived(slot):
-        remote(
-            lead_send.at[0], lead_chain.at[slot], lz_s.at[0], lz_r.at[slot], flip_y
-        ).wait_recv()
+        ref = lead_rows(lead_chain, slot)
+        remote(ref, ref, lz_s.at[0], lz_r.at[slot], flip_y).wait_recv()
 
     def z_arrived(slot, h):
         remote(
@@ -214,65 +233,35 @@
         make().start()
         sends[inside].append(make)
 
-    loads[1].wait()
-    loads[2].wait()
-
-    def multiply(i, carry):
-        at = pl.multiple_of(block_at(i) * pair, 128)
-        flipped[...] = attn[:, pl.ds(at, pair)].T
-        for h in range(pieces):
-            product = jnp.dot(flipped[...], cot[:, piece(h)], preferred_element_type=f32)
-            upper, lower = product[:rows], product[rows:]
-            own[i, :, piece(h)] = jnp.where(y == 0, upper, lower)
-            across = jnp.where(y == 0, lower, upper)
+    def multiply(i, h):
+        if h == 0:
+            attn_in[i].wait()
+            flipped[...] = attn[i].T
+        if i == 0:
+            cot_in[h].wait()
+        product = jnp.dot(flipped[...], cot[:, piece(h)], preferred_element_type=f32)
+        upper, lower = product[:rows], product[rows:]
+        across = jnp.where(y == 0, lower, upper)
+        if h < pieces or i == 2:
             psend[i, :, piece(h)] = across.astype(bf16)
-
-            @pl.when(i == last)
-            def _():
-                other[:, piece(h)] = across
-
-            early = jnp.where(inner, i == 0, i < last if h == 0 else i <= last)
-
-            @pl.when(early)
-            def _():
-                y_copy(i, h).start()
-
-            if h == 0:
-                @pl.when(jnp.logical_and(inner, i == 2))
-                def _():
-                    extra_copy(h).start()
-
-        lead_own[i] = jnp.dot(flipped[...], cot[:, :lead], preferred_element_type=f32)
-
-        @pl.when(jnp.logical_and(jnp.logical_not(inner), i < last))
-        def _():
-            lead_send[i] = lead_own[i].astype(bf16)
-
-            @pl.when(i < 2)
-            def _():
-                lead_copy(False, i).start()
-
-        return carry
-
-    lax.fori_loop(0, depth, multiply, 0)
-    for h in range(pieces):
-        sends[True].append(functools.partial(y_copy, 0, h))
-        for i in range(depth if h else last):
-            sends[False].append(functools.partial(y_copy, i, h))
-    sends[True].append(functools.partial(extra_copy, 0))
-    for i in range(2):
-        sends[False].append(functools.partial(lead_copy, False, i))
-
-    loads[3].wait()
-    loads[4].wait()
-    for k in range(1, groups):
-        parts[k - 1].wait_recv()
-    mine = pl.ds(pl.multiple_of(r * cols, 128), cols)
-    total = change[:, mine]
-    for k in range(1, groups):
-        total = total + got[k - 1].astype(f32)
-    summed_ref[...] = total
-    weights[f, :, mine] = outer_step(anchor[...], momentum[...], total, groups)[0].astype(bf16)
+        if h == pieces:
+            lead_own[i] = product
+            return
+        own[i, :, piece(h)] = jnp.where(y == 0, upper, lower)
+        if i == last and h < extras:
+            other[:, piece(h)] = across
+
+    def outer():
+        for copy in outer_in:
+            copy.wait()
+        for copy in parts:
+            copy.wait_recv()
+        mine = pl.ds(pl.multiple_of(r * cols, 128), cols)
+        total = change[:, mine]
+        for k in range(1, groups):
+            total = total + got[k - 1].astype(f32)
+        summed_ref[...] = total
+        weights[f, :, mine] = outer_step(anchor[...], momentum[...], total, groups)[0].astype(bf16)
 
     def shard_copy(where, index, device):
         zs, ys, xs, cs = where
@@ -293,20 +282,28 @@
             used[inside] += 1
 
     def lead_step(inside, i):
+        slot = i if i < 2 else depth - 1
         if inside:
-            slot = i if i < 2 else depth - 1
             lead_arrived(slot)
-
-            def add(there):
-                lead_send[i, there] = (
-                    lead_own[i, there] + lead_chain[slot, there].astype(f32)
-                ).astype(bf16)
-
-            by_rows(add, pair)
+        elif i == 2:
+            y_copy(i, pieces).wait_recv()
+            lead_send[i, pl.ds(home, rows)] = (
+                lead_own[i, pl.ds(home, rows)] + ry[i, :, piece(pieces)].astype(f32)
+            ).astype(bf16)
+            start(inside, functools.partial(lead_copy, inside, i))
+            return
+
+        def add(there):
+            value = lead_own[i, there]
+            if inside:
+                value = value + lead_chain[slot, there].astype(f32)
+            lead_send[i, there] = value.astype(bf16)
+
+        by_rows(add, pair)
         start(inside, functools.partial(lead_copy, inside, i))
 
     def chain_step(inside, i, h):
-        crossed = not inside or i < 2 or h > 0
+        crossed = not inside or i < 2 or h >= extras
         slot = i if i < 2 else depth - 1
         if crossed:
             y_copy(i, h).wait_recv()
@@ -340,20 +337,19 @@
     def lead_swap():
         return remote(lead_out, lead_in, ly_s.at[0], ly_r.at[0], flip_y)
 
-    away = pl.multiple_of((1 - y) * rows, 8)
-    home = pl.multiple_of(y * rows, 8)
 
     def cross_lead(inside):
-        for slot in ends[inside]:
-            lead_arrived(slot)
-        value = lead_own[last, pl.ds(away, rows)]
-        for slot in ends[inside]:
-            value = value + lead_chain[slot, pl.ds(away, rows)].astype(f32)
-        lead_out[...] = value.astype(bf16)
+        slot = ends[inside][-1]
+        lead_arrived(slot)
+        lead_out[...] = (
+            lead_own[last, pl.ds(away, rows)] + lead_chain[slot, pl.ds(away, rows)].astype(f32)
+        ).astype(bf16)
         start(inside, lead_swap)
 
     def finish_lead(inside):
         lead_swap().wait_recv()
+        if inside:
+            lead_arrived(2)
         value = lead_own[last, pl.ds(home, rows)] + lead_in[...].astype(f32)
         for slot in ends[inside]:
             value = value + lead_chain[slot, pl.ds(home, rows)].astype(f32)
@@ -390,8 +386,11 @@
             lead_step(inside, int(spot))
         elif kind == "S":
             chain_step(inside, int(spot[0]), int(spot[1]))
+        elif kind == "E":
+            start(inside, functools.partial(extra_copy, int(spot)))
         elif kind == "y":
-            start(inside, functools.partial(y_copy, int(spot[0]), int(spot[1])))
+            i, h = (2, pieces) if step == "yL" else (int(spot[0]), int(spot[1]))
+            start(inside, functools.partial(y_copy, i, h))
         elif step == "CL":
             cross_lead(inside)
         elif kind == "C":
@@ -401,25 +400,32 @@
         elif kind == "F":
             finish(inside, int(spot))
 
-    runs, outs = {}, {}
+    runs, joint = {True: [[]], False: [[]]}, {True: [], False: []}
     for inside, steps in ((True, INNER_STEPS), (False, OUTER_STEPS)):
-        runs[inside], outs[inside] = [[]], []
         for step in steps:
-            if step[0] == "M":
-                outs[inside].append(places[inside][step[1]])
+            if step[0] in "BWM":
+                joint[inside].append(step)
                 runs[inside].append([])
             else:
                 runs[inside][-1].append(step)
 
-    for k in range(depth + 1):
+    for k in range(len(joint[True]) + 1):
         for inside in (True, False):
-            @pl.when(inner if inside else jnp.logical_not(inner))
-            def _():
-                for step in runs[inside][k]:
-                    take(inside, step)
-
-        if k < depth:
-            zs = jnp.where(inner, outs[True][k], outs[False][k])
+            if runs[inside][k]:
+                @pl.when(inner if inside else jnp.logical_not(inner))
+                def _():
+                    for step in runs[inside][k]:
+                        take(inside, step)
+
+        if k == len(joint[True]):
+            continue
+        step = joint[True][k]
+        if step[0] == "B":
+            multiply(int(step[1]), pieces if step[2] == "L" else int(step[2]))
+        elif step[0] == "W":
+            outer()
+        else:
+            zs = jnp.where(inner, *(places[inside][joint[inside][k][1]] for inside in (True, False)))
             for ys in range(2):
                 for xs in range(2):
                     arrived((zs, ys, xs, 1 - core))
@@ -474,8 +480,8 @@
 
 def plan(width):
     lead = width // 6 // 128 * 128
-    half = (width - lead) // 256 * 128
-    return lead, ((lead, half), (lead + half, width - lead - half))
+    part = width // 2 // 128 * 128
+    return lead, ((lead, part), (lead + part, width - lead - part)), 1
 
 
 def fused_shards(anchor, momentum, change, adam_first, adam_second, attn_out, grad_out):
@@ -484,7 +490,7 @@
     rows, width = change.shape[1:]
     tokens = attn_out.shape[1]
     cols = width // groups
-    lead, cuts = plan(width)
+    lead, cuts, extras = plan(width)
     rest = width - lead
     pieces = len(cuts)
     scale = (tokens * devices) ** (-0.5)
@@ -493,7 +499,7 @@
     in_hbm = pl.BlockSpec(memory_space=pltpu.HBM)
     in_vmem = pl.BlockSpec(memory_space=pltpu.VMEM)
     summed, anchor_row, gradient, input_grad = pl.pallas_call(
-        functools.partial(kernel, depth, groups, scale, lead, cuts),
+        functools.partial(kernel, depth, groups, scale, lead, cuts, extras),
         out_shape=(
             jax.ShapeDtypeStruct((rows, cols), f32),
             jax.ShapeDtypeStruct((rows, width), bf16),
@@ -506,7 +512,7 @@
             vmem((rows, cols), f32),
             vmem((rows, cols), f32),
             vmem((rows, width), f32),
-            vmem((tokens, width), bf16),
+            vmem((depth, tokens, 2 * rows), bf16),
             vmem((tokens, width), bf16),
             vmem((2 * rows, tokens), bf16),
             vmem((groups, rows, cols), bf16),
@@ -523,9 +529,9 @@
             vmem((depth + 1, 2 * rows, lead), bf16),
             vmem((rows, lead), bf16),
             vmem((rows, lead), bf16),
-            dma((5,)),
+            dma((depth + pieces + 4,)),
             dma((groups - 1,)), dma((groups - 1,)),
-            dma((depth * pieces,)), dma((depth * pieces,)),
+            dma((depth * (pieces + 1),)), dma((depth * (pieces + 1),)),
             dma((depth * pieces,)), dma(((depth + 1) * pieces,)),
             dma((depth - 1,)), dma((depth + 1,)), dma((1,)), dma((1,)),
             dma((5 * devices,)), dma((groups * devices,)),

time: 62.9 us -> 59.9 us (0.952)
  the two profiles are of different devices: /device:TPU:14 before, /device:TPU:0 now
where the time goes in v2:
time: 59.9 us; the launch traced here: 59.7 us
  Pallas kernels  59 us (98%)
  between operations  0.71 us (1%)
    pallas_call x1, Pallas kernels, fused_shards(): pl.pallas_call(functools.partial(kernel, depth, groups, scale, lead, cuts...  55.9 us
    pallas_call x1, Pallas kernels, fused_shards(): pl.pallas_call(functools.partial(finish_kernel, groups, lines), out_shape...  3.07 us

profile of v2, /device:TPU:0, one launch (start us, length us, event | category | flops | bytes accessed | tf_op | source)
XLA Modules:
  0.0 59.7 jit_solution(18002228792993998234)
XLA Ops:
  0.6 0.0 copy-start
  0.6 0.0 copy-start.1
  0.7 0.0 copy-start.2
  0.7 0.0 copy-start.3
  0.7 55.9 %shard_map.118 = (f32[192,384]{1,0:T(8,128)S(1)}, bf16[192,1536]{1,0:T(8,128)(2,1)S(1)}, f32[192,1536]{1,0:T(8,128)S(1)}, bf16[1024,1536]{1,0:T(8,128)(2,1)S(1)}) custom-call(f32[192,384]{1,0:T(8,128)} %anchor.1, f32[192,384]{1,0:T(8,128)} %momentum.1, f32[192,1536]{1,0:T(8,128)} %bitcast.13, bf16[1024,1536]{1,0:T(8,128)(2,1)} %bitcast.11, ...), custom_call_target="tpu_custom_call" | custom-call | tf_op jit(solution)/shard_map/pallas_call | solution.py:501
  56.6 0.0 copy-done
  56.6 0.0 copy-done.1
  56.6 0.0 copy-done.2
  56.6 0.0 copy-done.3
  56.6 3.1 %shard_map.119 = (f32[192,384]{1,0:T(8,128)}, f32[192,384]{1,0:T(8,128)}, f32[192,1536]{1,0:T(8,128)}, f32[192,1536]{1,0:T(8,128)}, f32[192,1536]{1,0:T(8,128)}, /*index=5*/bf16[1024,1536]{1,0:T(8,128)(2,1)}) custom-call(f32[192,384]{1,0:T(8,128)S(1)} %copy-done, f32[192,384]{1,0:T(8,128)S(1)} %copy-done.1, f32[192,384]{1,0:T(8,128)S(1)} %get-tuple-element.16.summed, ...), custom_call_target="tpu_custom_call" | custom-call | tf_op jit(solution)/shard_map/pallas_call | solution.py:549
Async XLA Ops:
  0.6 56.0 %copy-start = (f32[192,384]{1,0:T(8,128)S(1)}, f32[192,384]{1,0:T(8,128)}, u32[]{:S(2)}) copy-start(f32[192,384]{1,0:T(8,128)} %anchor.1) | copy-start | bytes 884740
  0.6 56.0 %copy-start.1 = (f32[192,384]{1,0:T(8,128)S(1)}, f32[192,384]{1,0:T(8,128)}, u32[]{:S(2)}) copy-start(f32[192,384]{1,0:T(8,128)} %momentum.1) | copy-start | bytes 884740
  0.7 56.0 %copy-start.2 = (f32[1,192,1536]{2,1,0:T(8,128)S(1)}, f32[1,192,1536]{2,1,0:T(8,128)}, u32[]{:S(2)}) copy-start(f32[1,192,1536]{2,1,0:T(8,128)} %param.10) | copy-start | bytes 3538948
  0.7 56.0 %copy-start.3 = (f32[1,192,1536]{2,1,0:T(8,128)S(1)}, f32[1,192,1536]{2,1,0:T(8,128)}, u32[]{:S(2)}) copy-start(f32[1,192,1536]{2,1,0:T(8,128)} %param.11) | copy-start | bytes 3538948

commit v3 on v2

--- a/solution.py
+++ b/solution.py
@@ -60,16 +60,16 @@
 
 
 INNER_STEPS = (
-    "B00", "y00", "B0L", "B01", "B10", "B1L", "B11", "B20", "y01", "E0", "B2L", "B21", "B30", "L0", "B3L",
-    "B31", "W", "own", "y11", "L2", "aa0", "ao1", "ac0", "L1", "ab0", "xo0", "S00", "y10", "ab1", "S01",
-    "aa1", "xc0", "xa0", "ac1", "xo1", "y21", "xb0", "y31", "Mo", "S11", "xa1", "S20", "xb1", "y30", "S10",
-    "CL", "Mb", "S21", "xc1", "Ma", "Mc", "F0", "F1", "FL",
+    "B00", "y00", "P", "B0L", "B01", "B10", "R", "E0", "B1L", "B11", "B20", "y01", "B2L", "B21", "B30",
+    "L0", "B3L", "B31", "W", "own", "y11", "L2", "aa0", "ao1", "ac0", "L1", "ab0", "xo0", "S00", "y10",
+    "ab1", "S01", "aa1", "xc0", "xa0", "ac1", "xo1", "y21", "xb0", "y31", "Mo", "S11", "xa1", "S20", "xb1",
+    "y30", "CL", "Mb", "S10", "S21", "xc1", "Ma", "Mc", "F0", "F1", "FL",
 )
 OUTER_STEPS = (
-    "B00", "y00", "B0L", "L0", "B01", "B10", "B1L", "B11", "B20", "L1", "B2L", "y01", "B21", "B30", "B3L",
-    "B31", "W", "own", "yL", "S00", "y11", "y10", "y20", "S01", "ab0", "xo0", "L2", "ab1", "S11", "ad0",
-    "CL", "S10", "y21", "ac0", "xb1", "S20", "xb0", "ac1", "C0", "FL", "ao1", "Mb", "xc1", "S21", "ad1",
-    "y31", "xc0", "xd0", "xo1", "Mc", "xd1", "Mo", "F0", "Md", "F1",
+    "B00", "y00", "P", "B0L", "L0", "B01", "B10", "R", "B1L", "B11", "B20", "L1", "B2L", "y01", "B21",
+    "B30", "B3L", "B31", "W", "own", "S00", "y11", "y10", "y20", "S01", "L2", "ab0", "S11", "xo0", "ab1",
+    "ad0", "CL", "S10", "y21", "ac0", "xb1", "S20", "xb0", "ac1", "C0", "FL", "ao1", "Mb", "xc1", "S21",
+    "ad1", "y31", "xc0", "xd0", "xo1", "Mc", "xd1", "Mo", "F0", "Md", "F1",
 )
 ROUTES = {
     True: {"o0": "bayxs", "a0": "ybxs", "o1": "abxs", "a1": "axs", "c0": "yaxs"},
@@ -120,8 +120,11 @@
         upper = jnp.where(i < z, i, last - (i - z))
         return jnp.where(low, lower, upper)
 
-    def block_columns(i):
-        return pl.ds(pl.multiple_of(block_at(i) * pair, 128), pair)
+    def block_order(k):
+        return jnp.where(inner, 3 - k, k) if 0 < k < last else k
+
+    def block_columns(k):
+        return pl.ds(pl.multiple_of(block_at(block_order(k)) * pair, 128), pair)
 
     def piece(h):
         return pl.ds(*cuts[h]) if h < pieces else pl.ds(0, lead)
@@ -160,18 +163,24 @@
             device_id=device, device_id_type=MESH,
         )
 
-    change_in.wait()
-    for k in range(1, groups):
-        at = pl.multiple_of(((r + k) % groups) * cols, 128)
-        part[k] = change[:, pl.ds(at, cols)].astype(bf16)
-    pl.semaphore_wait(barrier, groups + 1 + jnp.where(inner, 1, 0))
-    parts = []
-    for k in range(1, groups):
-        parts.append(remote(
-            part.at[k], got.at[k - 1], part_s.at[k - 1], part_r.at[k - 1],
-            {"replica": (r + k) % groups, "fsdp": f},
-        ))
-        parts[-1].start()
+    def quarter(xs, cs):
+        return pl.ds(pl.multiple_of((xs * 2 + cs) * cols, 128), cols)
+
+    def part_copy(k):
+        return remote(
+            part.at[k], got.at[k], part_s.at[k], part_r.at[k], links["s" if k < 2 else "x"]
+        )
+
+    def send_parts():
+        change_in.wait()
+        for k, xs in ((1, over_x), (0, x)):
+            part[k] = change[:, quarter(xs, 1 - core)].astype(bf16)
+            part_copy(k).start()
+
+    def relay_parts():
+        part_copy(1).wait_recv()
+        part[2] = (change[:, quarter(over_x, core)] + got[1].astype(f32)).astype(bf16)
+        part_copy(2).start()
 
     lines = 16
 
@@ -185,7 +194,7 @@
     def y_copy(i, h):
         return remote(
             psend.at[i, :, piece(h)], ry.at[i, :, piece(h)],
-            py_s.at[(pieces + 1) * i + h], py_r.at[(pieces + 1) * i + h], flip_y,
+            py_s.at[pieces * i + h], py_r.at[pieces * i + h], flip_y,
         )
 
     def route(inside, i):
@@ -196,13 +205,9 @@
     away = pl.multiple_of((1 - y) * rows, 16)
     home = pl.multiple_of(y * rows, 16)
 
-    def lead_rows(ref, slot):
-        return ref.at[slot, pl.ds(home, rows)] if slot == 2 else ref.at[slot]
-
     def lead_copy(inside, i):
         slot, device = route(inside, i)
-        src = lead_send.at[i] if inside else lead_rows(lead_send, i)
-        return remote(src, lead_rows(lead_chain, slot), lz_s.at[i], lz_r.at[slot], device)
+        return remote(lead_send.at[i], lead_chain.at[slot], lz_s.at[i], lz_r.at[slot], device)
 
     def z_copy(inside, i, h):
         slot, device = route(inside, i)
@@ -218,7 +223,7 @@
         )
 
     def lead_arrived(slot):
-        ref = lead_rows(lead_chain, slot)
+        ref = lead_chain.at[slot]
         remote(ref, ref, lz_s.at[0], lz_r.at[slot], flip_y).wait_recv()
 
     def z_arrived(slot, h):
@@ -233,33 +238,31 @@
         make().start()
         sends[inside].append(make)
 
-    def multiply(i, h):
+    def multiply(k, h):
+        i = block_order(k)
         if h == 0:
-            attn_in[i].wait()
-            flipped[...] = attn[i].T
-        if i == 0:
+            attn_in[k].wait()
+            flipped[...] = attn[k].T
+        if k == 0:
             cot_in[h].wait()
         product = jnp.dot(flipped[...], cot[:, piece(h)], preferred_element_type=f32)
-        upper, lower = product[:rows], product[rows:]
-        across = jnp.where(y == 0, lower, upper)
-        if h < pieces or i == 2:
-            psend[i, :, piece(h)] = across.astype(bf16)
         if h == pieces:
             lead_own[i] = product
             return
+        upper, lower = product[:rows], product[rows:]
+        across = jnp.where(y == 0, lower, upper)
+        psend[i, :, piece(h)] = across.astype(bf16)
         own[i, :, piece(h)] = jnp.where(y == 0, upper, lower)
-        if i == last and h < extras:
+        if k == last and h < extras:
             other[:, piece(h)] = across
 
     def outer():
         for copy in outer_in:
             copy.wait()
-        for copy in parts:
-            copy.wait_recv()
-        mine = pl.ds(pl.multiple_of(r * cols, 128), cols)
-        total = change[:, mine]
-        for k in range(1, groups):
-            total = total + got[k - 1].astype(f32)
+        mine = quarter(x, core)
+        part_copy(0).wait_recv()
+        part_copy(2).wait_recv()
+        total = change[:, mine] + got[0].astype(f32) + got[2].astype(f32)
         summed_ref[...] = total
         weights[f, :, mine] = outer_step(anchor[...], momentum[...], total, groups)[0].astype(bf16)
 
@@ -285,13 +288,6 @@
         slot = i if i < 2 else depth - 1
         if inside:
             lead_arrived(slot)
-        elif i == 2:
-            y_copy(i, pieces).wait_recv()
-            lead_send[i, pl.ds(home, rows)] = (
-                lead_own[i, pl.ds(home, rows)] + ry[i, :, piece(pieces)].astype(f32)
-            ).astype(bf16)
-            start(inside, functools.partial(lead_copy, inside, i))
-            return
 
         def add(there):
             value = lead_own[i, there]
@@ -339,17 +335,15 @@
 
 
     def cross_lead(inside):
-        slot = ends[inside][-1]
-        lead_arrived(slot)
-        lead_out[...] = (
-            lead_own[last, pl.ds(away, rows)] + lead_chain[slot, pl.ds(away, rows)].astype(f32)
-        ).astype(bf16)
+        value = lead_own[last, pl.ds(away, rows)]
+        for slot in ends[inside]:
+            lead_arrived(slot)
+            value = value + lead_chain[slot, pl.ds(away, rows)].astype(f32)
+        lead_out[...] = value.astype(bf16)
         start(inside, lead_swap)
 
     def finish_lead(inside):
         lead_swap().wait_recv()
-        if inside:
-            lead_arrived(2)
         value = lead_own[last, pl.ds(home, rows)] + lead_in[...].astype(f32)
         for slot in ends[inside]:
             value = value + lead_chain[slot, pl.ds(home, rows)].astype(f32)
@@ -389,8 +383,7 @@
         elif kind == "E":
             start(inside, functools.partial(extra_copy, int(spot)))
         elif kind == "y":
-            i, h = (2, pieces) if step == "yL" else (int(spot[0]), int(spot[1]))
-            start(inside, functools.partial(y_copy, i, h))
+            start(inside, functools.partial(y_copy, int(spot[0]), int(spot[1])))
         elif step == "CL":
             cross_lead(inside)
         elif kind == "C":
@@ -403,7 +396,7 @@
     runs, joint = {True: [[]], False: [[]]}, {True: [], False: []}
     for inside, steps in ((True, INNER_STEPS), (False, OUTER_STEPS)):
         for step in steps:
-            if step[0] in "BWM":
+            if step[0] in "BPRWM":
                 joint[inside].append(step)
                 runs[inside].append([])
             else:
@@ -422,6 +415,12 @@
         step = joint[True][k]
         if step[0] == "B":
             multiply(int(step[1]), pieces if step[2] == "L" else int(step[2]))
+            if step == "B00":
+                pl.semaphore_wait(barrier, groups + 1 + jnp.where(inner, 1, 0))
+        elif step[0] == "P":
+            send_parts()
+        elif step[0] == "R":
+            relay_parts()
         elif step[0] == "W":
             outer()
         else:
@@ -429,15 +428,16 @@
             for ys in range(2):
                 for xs in range(2):
                     arrived((zs, ys, xs, 1 - core))
+            if k == len(joint[True]) - 1:
+                row_ref[...] = weights[f]
             there = pl.ds(pl.multiple_of(zs * pair, 128), pair)
             block = weights[pl.ds(2 * zs, 2)].reshape(pair, width)
             back[:, there] = lax.dot_general(
                 cot[...], block, (((1,), (1,)), ((), ())), preferred_element_type=f32
             ).astype(bf16)
 
-    row_ref[...] = weights[f]
-    for copy in parts:
-        copy.wait_send()
+    for k in range(3):
+        part_copy(k).wait_send()
     for inside in (True, False):
         @pl.when(inner if inside else jnp.logical_not(inner))
         def _():
@@ -515,8 +515,8 @@
             vmem((depth, tokens, 2 * rows), bf16),
             vmem((tokens, width), bf16),
             vmem((2 * rows, tokens), bf16),
-            vmem((groups, rows, cols), bf16),
-            vmem((groups - 1, rows, cols), bf16),
+            vmem((3, rows, cols), bf16),
+            vmem((3, rows, cols), bf16),
             vmem((depth, rows, width), f32),
             vmem((rows, width), f32),
             vmem((depth, rows, width), bf16),
@@ -530,8 +530,8 @@
             vmem((rows, lead), bf16),
             vmem((rows, lead), bf16),
             dma((depth + pieces + 4,)),
-            dma((groups - 1,)), dma((groups - 1,)),
-            dma((depth * (pieces + 1),)), dma((depth * (pieces + 1),)),
+            dma((3,)), dma((3,)),
+            dma((depth * pieces,)), dma((depth * pieces,)),
             dma((depth * pieces,)), dma(((depth + 1) * pieces,)),
             dma((depth - 1,)), dma((depth + 1,)), dma((1,)), dma((1,)),
             dma((5 * devices,)), dma((groups * devices,)),

time: 59.9 us -> 58.9 us (0.983)
  Pallas kernels: 59 us -> 58 us
    pallas_call x1, Pallas kernels: 55.9 us -> 54.9 us  [fused_shards(): pl.pallas_call(functools.partial(kernel, depth, groups, scale, lead, cuts...]
where the time goes in v3:
time: 58.9 us; the launch traced here: 58.7 us
  Pallas kernels  58 us (98%)
  between operations  0.71 us (1%)
    pallas_call x1, Pallas kernels, fused_shards(): pl.pallas_call(functools.partial(kernel, depth, groups, scale, lead, cuts...  54.9 us
    pallas_call x1, Pallas kernels, fused_shards(): pl.pallas_call(functools.partial(finish_kernel, groups, lines), out_shape...  3.07 us

profile of v3, /device:TPU:0, one launch (start us, length us, event | category | flops | bytes accessed | tf_op | source)
XLA Modules:
  0.0 58.7 jit_solution(11561197675078664801)
XLA Ops:
  0.6 0.0 copy-start
  0.6 0.0 copy-start.1
  0.7 0.0 copy-start.2
  0.7 0.0 copy-start.3
  0.7 54.9 %shard_map.118 = (f32[192,384]{1,0:T(8,128)S(1)}, bf16[192,1536]{1,0:T(8,128)(2,1)S(1)}, f32[192,1536]{1,0:T(8,128)S(1)}, bf16[1024,1536]{1,0:T(8,128)(2,1)S(1)}) custom-call(f32[192,384]{1,0:T(8,128)} %anchor.1, f32[192,384]{1,0:T(8,128)} %momentum.1, f32[192,1536]{1,0:T(8,128)} %bitcast.13, bf16[1024,1536]{1,0:T(8,128)(2,1)} %bitcast.11, ...), custom_call_target="tpu_custom_call" | custom-call | tf_op jit(solution)/shard_map/pallas_call | solution.py:501
  55.6 0.0 copy-done
  55.6 0.0 copy-done.1
  55.6 0.0 copy-done.2
  55.6 0.0 copy-done.3
  55.6 3.1 %shard_map.119 = (f32[192,384]{1,0:T(8,128)}, f32[192,384]{1,0:T(8,128)}, f32[192,1536]{1,0:T(8,128)}, f32[192,1536]{1,0:T(8,128)}, f32[192,1536]{1,0:T(8,128)}, /*index=5*/bf16[1024,1536]{1,0:T(8,128)(2,1)}) custom-call(f32[192,384]{1,0:T(8,128)S(1)} %copy-done, f32[192,384]{1,0:T(8,128)S(1)} %copy-done.1, f32[192,384]{1,0:T(8,128)S(1)} %get-tuple-element.16.summed, ...), custom_call_target="tpu_custom_call" | custom-call | tf_op jit(solution)/shard_map/pallas_call | solution.py:549
Async XLA Ops:
  0.6 55.0 %copy-start = (f32[192,384]{1,0:T(8,128)S(1)}, f32[192,384]{1,0:T(8,128)}, u32[]{:S(2)}) copy-start(f32[192,384]{1,0:T(8,128)} %anchor.1) | copy-start | bytes 884740
  0.6 55.0 %copy-start.1 = (f32[192,384]{1,0:T(8,128)S(1)}, f32[192,384]{1,0:T(8,128)}, u32[]{:S(2)}) copy-start(f32[192,384]{1,0:T(8,128)} %momentum.1) | copy-start | bytes 884740
  0.7 55.0 %copy-start.2 = (f32[1,192,1536]{2,1,0:T(8,128)S(1)}, f32[1,192,1536]{2,1,0:T(8,128)}, u32[]{:S(2)}) copy-start(f32[1,192,1536]{2,1,0:T(8,128)} %param.10) | copy-start | bytes 3538948
  0.7 55.0 %copy-start.3 = (f32[1,192,1536]{2,1,0:T(8,128)S(1)}, f32[1,192,1536]{2,1,0:T(8,128)}, u32[]{:S(2)}) copy-start(f32[1,192,1536]{2,1,0:T(8,128)} %param.11) | copy-start | bytes 3538948

commit v4 on v3

--- a/solution.py
+++ b/solution.py
@@ -146,12 +146,8 @@
     outer_in = (load(anchor_hbm, anchor), load(momentum_hbm, momentum))
 
     barrier = pltpu.get_barrier_semaphore()
-    for k in range(1, groups):
-        pl.semaphore_signal(
-            barrier, inc=1, device_id={"replica": (r + k) % groups, "fsdp": f}, device_id_type=MESH
-        )
-    pl.semaphore_signal(barrier, inc=1, device_id=flip_y, device_id_type=MESH)
-    pl.semaphore_signal(barrier, inc=1, device_id=to_inward, device_id_type=MESH)
+    for name in "sxyb":
+        pl.semaphore_signal(barrier, inc=1, device_id=links[name], device_id_type=MESH)
 
     @pl.when(inner)
     def _():
@@ -182,7 +178,7 @@
         part[2] = (change[:, quarter(over_x, core)] + got[1].astype(f32)).astype(bf16)
         part_copy(2).start()
 
-    lines = 16
+    lines = 32
 
     def by_rows(body, count):
         def step(j, carry):
@@ -416,7 +412,7 @@
         if step[0] == "B":
             multiply(int(step[1]), pieces if step[2] == "L" else int(step[2]))
             if step == "B00":
-                pl.semaphore_wait(barrier, groups + 1 + jnp.where(inner, 1, 0))
+                pl.semaphore_wait(barrier, 4 + jnp.where(inner, 1, 0))
         elif step[0] == "P":
             send_parts()
         elif step[0] == "R":

time: 58.9 us -> 58.9 us (level)
  no operation moved by 1% of the time
where the time goes in v4:
time: 58.9 us; the launch traced here: 58.7 us
  Pallas kernels  58 us (98%)
  between operations  0.71 us (1%)
    pallas_call x1, Pallas kernels, fused_shards(): pl.pallas_call(functools.partial(kernel, depth, groups, scale, lead, cuts...  54.9 us
    pallas_call x1, Pallas kernels, fused_shards(): pl.pallas_call(functools.partial(finish_kernel, groups, lines), out_shape...  3.07 us

profile of v4, /device:TPU:0, one launch (start us, length us, event | category | flops | bytes accessed | tf_op | source)
XLA Modules:
  0.0 58.7 jit_solution(10977747386612723201)
XLA Ops:
  0.6 0.0 copy-start
  0.6 0.0 copy-start.1
  0.7 0.0 copy-start.2
  0.7 0.0 copy-start.3
  0.7 54.9 %shard_map.118 = (f32[192,384]{1,0:T(8,128)S(1)}, bf16[192,1536]{1,0:T(8,128)(2,1)S(1)}, f32[192,1536]{1,0:T(8,128)S(1)}, bf16[1024,1536]{1,0:T(8,128)(2,1)S(1)}) custom-call(f32[192,384]{1,0:T(8,128)} %anchor.1, f32[192,384]{1,0:T(8,128)} %momentum.1, f32[192,1536]{1,0:T(8,128)} %bitcast.13, bf16[1024,1536]{1,0:T(8,128)(2,1)} %bitcast.11, ...), custom_call_target="tpu_custom_call" | custom-call | tf_op jit(solution)/shard_map/pallas_call | solution.py:497
  55.6 0.0 copy-done
  55.6 0.0 copy-done.1
  55.6 0.0 copy-done.2
  55.6 0.0 copy-done.3
  55.7 3.1 %shard_map.119 = (f32[192,384]{1,0:T(8,128)}, f32[192,384]{1,0:T(8,128)}, f32[192,1536]{1,0:T(8,128)}, f32[192,1536]{1,0:T(8,128)}, f32[192,1536]{1,0:T(8,128)}, /*index=5*/bf16[1024,1536]{1,0:T(8,128)(2,1)}) custom-call(f32[192,384]{1,0:T(8,128)S(1)} %copy-done, f32[192,384]{1,0:T(8,128)S(1)} %copy-done.1, f32[192,384]{1,0:T(8,128)S(1)} %get-tuple-element.16.summed, ...), custom_call_target="tpu_custom_call" | custom-call | tf_op jit(solution)/shard_map/pallas_call | solution.py:545
Async XLA Ops:
  0.6 55.0 %copy-start = (f32[192,384]{1,0:T(8,128)S(1)}, f32[192,384]{1,0:T(8,128)}, u32[]{:S(2)}) copy-start(f32[192,384]{1,0:T(8,128)} %anchor.1) | copy-start | bytes 884740
  0.6 55.0 %copy-start.1 = (f32[192,384]{1,0:T(8,128)S(1)}, f32[192,384]{1,0:T(8,128)}, u32[]{:S(2)}) copy-start(f32[192,384]{1,0:T(8,128)} %momentum.1) | copy-start | bytes 884740
  0.7 55.0 %copy-start.2 = (f32[1,192,1536]{2,1,0:T(8,128)S(1)}, f32[1,192,1536]{2,1,0:T(8,128)}, u32[]{:S(2)}) copy-start(f32[1,192,1536]{2,1,0:T(8,128)} %param.10) | copy-start | bytes 3538948
  0.7 55.0 %copy-start.3 = (f32[1,192,1536]{2,1,0:T(8,128)S(1)}, f32[1,192,1536]{2,1,0:T(8,128)}, u32[]{:S(2)}) copy-start(f32[1,192,1536]{2,1,0:T(8,128)} %param.11) | copy-start | bytes 3538948
